TPU v7x, 32 devices: a whole 2x2x4 slice. The times are simulated.
32 devices in a mesh: dp: 8 (over y, x, core), tensor: 4 (over z).
Axes of the slice: x: 2, y: 2, z: 4, core: 2. Of those that a mesh axis runs over, the one named last changes fastest.
Arguments:
- inputs: bfloat16 [4, 4096, 768], P(None, ('dp', 'tensor')), may hold values from -12 to 12
- cotangent: bfloat16 [4, 4096, 768], P(None, ('dp', 'tensor')), may hold values from -12 to 12
- segment_ids: int32 [4, 8, 512], P(None, 'dp'), may hold values from 0 to 23, never falling along the last dimension, each value on 1 to 48 neighbouring positions
- ln1_gain: float32 [768], replicated, may hold values from 0.25 to 1.75
- ln1_bias: float32 [768], replicated, may hold values from -1.75 to 1.75
- qkv_weight: bfloat16 [3, 768, 768], P(None, 'dp', 'tensor'), may hold values from -0.21875 to 0.21875
- qv_bias: float32 [2, 768], P(None, 'tensor'), may hold values from -1.75 to 1.75
- out_weight: bfloat16 [768, 768], P('tensor', 'dp'), may hold values from -0.4375 to 0.4375
- out_bias: float32 [768], replicated, may hold values from -1.75 to 1.75
- ln2_gain: float32 [768], replicated, may hold values from 0.25 to 1.75
- ln2_bias: float32 [768], replicated, may hold values from -1.75 to 1.75
- up_weight: bfloat16 [768, 3072], P('dp', 'tensor'), may hold values from -0.21875 to 0.21875
- up_bias: float32 [3072], P('tensor'), may hold values from -1.75 to 1.75
- down_weight: bfloat16 [3072, 768], P('tensor', 'dp'), may hold values from -0.109375 to 0.109375
- down_bias: float32 [768], replicated, may hold values from -1.75 to 1.75
Outputs:
- outputs: float32 [4, 4096, 768], P(None, ('dp', 'tensor'))
- input_grad: float32 [4, 4096, 768], P(None, ('dp', 'tensor'))
- ln1_gain_grad: float32 [768], replicated
- ln1_bias_grad: float32 [768], replicated
- qkv_weight_grad: float32 [3, 768, 768], P(None, 'dp', 'tensor')
- qv_bias_grad: float32 [2, 768], replicated
- out_weight_grad: float32 [768, 768], P('tensor', 'dp')
- out_bias_grad: float32 [768], replicated
- ln2_gain_grad: float32 [768], replicated
- ln2_bias_grad: float32 [768], replicated
- up_weight_grad: float32 [768, 3072], P('dp', 'tensor')
- up_bias_grad: float32 [3072], replicated
- down_weight_grad: float32 [3072, 768], P('tensor', 'dp')
- down_bias_grad: float32 [768], replicated
Inputs may be any that keep to these rules, and one draw needn't show every extreme that they name: `segment_ids`: along each sequence of 512 tokens the ids never fall; a caption spans 1 to 48 tokens, and one caption of each sequence exactly 48.
All inputs are finite; a program needn't handle non-finite values.
Results may differ from a plain program's by a relative error of at most 0.017.
Values may be sent and summed in bfloat16 or wider, within the bound.
A program may use at most 192 MiB of HBM per device.

v0:
```python
import jax
import jax.numpy as jnp
from jax import lax
from jax.sharding import PartitionSpec as P

HD = 64
epsilon = 1e-05
masked_value = -1000000000.0


def layer_norm(stream_values, scales, shifts):
    centered = stream_values - jnp.mean(stream_values, -1, keepdims=True)
    variance = jnp.mean(centered * centered, -1, keepdims=True)
    return centered * lax.rsqrt(variance + epsilon) * scales + shifts


def gelu_exact(hidden):
    return jax.nn.gelu(hidden, approximate=False)


def contract(operand_left, operand_right, left_dim, right_dim):
    return lax.dot_general(
        operand_left,
        operand_right,
        (((left_dim,), (right_dim,)), ((), ())),
        preferred_element_type=jnp.float32,
    )


def gather_rows(values_low):
    return lax.all_gather(values_low, "tensor", axis=0, tiled=True)


def gather_grads(values_low):
    return lax.all_gather(values_low, "tensor", axis=0, tiled=True)


def rows_sum(operand_left, operand_right, einsum_form):
    return lax.psum_scatter(
        jnp.einsum(
            einsum_form, operand_left, operand_right, preferred_element_type=jnp.float32
        ).astype(jnp.bfloat16),
        "tensor",
        scatter_dimension=0,
        tiled=True,
    ).astype(jnp.float32)


def grads_sum(operand_left, operand_right, einsum_form):
    return lax.psum_scatter(
        jnp.einsum(
            einsum_form, operand_left, operand_right, preferred_element_type=jnp.float32
        ).astype(jnp.bfloat16),
        "tensor",
        scatter_dimension=0,
        tiled=True,
    ).astype(jnp.float32)


def scores_of(query_heads, key_heads, same_caption):
    raw_scores = jnp.einsum(
        "bqhd,bkhd->bhqk", query_heads, key_heads, preferred_element_type=jnp.float32
    )
    return jnp.where(same_caption, raw_scores * HD ** (-0.5), masked_value)


def body(
    inputs,
    cotangent,
    segment_ids,
    ln1_gain,
    ln1_bias,
    qkv_weight,
    qv_bias,
    out_weight,
    out_bias,
    ln2_gain,
    ln2_bias,
    up_weight,
    up_bias,
    down_weight,
    down_bias,
):
    batches, shard_rows, model_width = inputs.shape
    sequences, seq_length = (segment_ids.shape[1], segment_ids.shape[2])
    head_cols = qkv_weight.shape[2]
    local_heads = head_cols // HD
    hidden_local = up_weight.shape[1]
    full_rows = sequences * seq_length
    shape_heads = (sequences, seq_length, local_heads, HD)
    tensor_pos = lax.axis_index("tensor")
    zero_index = tensor_pos * 0
    full_grads = (
        jnp.zeros((3, model_width, head_cols), jnp.float32),
        jnp.zeros((head_cols, model_width), jnp.float32),
        jnp.zeros((model_width, hidden_local), jnp.float32),
        jnp.zeros((hidden_local, model_width), jnp.float32),
    )
    qv_total = jnp.zeros((2, head_cols), jnp.float32)
    up_total = jnp.zeros((hidden_local,), jnp.float32)
    out_total = jnp.zeros((model_width,), jnp.float32)
    down_total = jnp.zeros((model_width,), jnp.float32)
    gain1_total = jnp.zeros((model_width,), jnp.float32)
    shift1_total = jnp.zeros((model_width,), jnp.float32)
    gain2_total = jnp.zeros((model_width,), jnp.float32)
    shift2_total = jnp.zeros((model_width,), jnp.float32)
    result_list = []
    input_list = []
    for micro_index in range(batches):
        weights_now = (
            lax.all_gather(qkv_weight, "dp", axis=1, tiled=True),
            lax.all_gather(out_weight, "dp", axis=1, tiled=True),
            lax.all_gather(up_weight, "dp", axis=0, tiled=True),
            lax.all_gather(down_weight, "dp", axis=1, tiled=True),
        )
        qkv_full, out_full, up_full, down_full = weights_now
        segment_now = segment_ids[micro_index]
        same_caption = (segment_now[:, :, None] == segment_now[:, None, :])[:, None]
        stream = inputs[micro_index].astype(jnp.float32)
        normed, norm_pull = jax.vjp(layer_norm, stream, ln1_gain, ln1_bias)
        normed_rows = gather_rows(normed.astype(jnp.bfloat16))
        query_heads = (
            (contract(normed_rows, qkv_full[0], 1, 0) + qv_bias[0])
            .astype(jnp.bfloat16)
            .reshape(shape_heads)
        )
        key_heads = (
            contract(normed_rows, qkv_full[1], 1, 0).astype(jnp.bfloat16).reshape(shape_heads)
        )
        value_heads = (
            (contract(normed_rows, qkv_full[2], 1, 0) + qv_bias[1])
            .astype(jnp.bfloat16)
            .reshape(shape_heads)
        )
        scores = scores_of(query_heads, key_heads, same_caption)
        row_top = jnp.max(scores, -1, keepdims=True)
        shifted = jnp.exp(scores - row_top)
        row_total = jnp.sum(shifted, -1, keepdims=True)
        log_total = row_top + jnp.log(row_total)
        probs_low = (shifted / row_total).astype(jnp.bfloat16)
        mixed = jnp.einsum(
            "bhqk,bkhd->bqhd", probs_low, value_heads, preferred_element_type=jnp.float32
        )
        mixed = mixed.reshape(full_rows, head_cols).astype(jnp.bfloat16)
        middle = stream + rows_sum(mixed, out_full, "sc,cd->sd") + out_bias
        normed_two, norm_two_pull = jax.vjp(layer_norm, middle, ln2_gain, ln2_bias)
        normed_two_rows = gather_rows(normed_two.astype(jnp.bfloat16))
        hidden = contract(normed_two_rows, up_full, 1, 0) + up_bias
        active, gelu_pull = jax.vjp(gelu_exact, hidden)
        active_low = active.astype(jnp.bfloat16)
        feed_out = rows_sum(active_low, down_full, "sc,cd->sd") + down_bias
        result_list.append(middle + feed_out)
        grad_stream = cotangent[micro_index].astype(jnp.float32)
        feed_grad = cotangent[micro_index]
        down_total = down_total + jnp.sum(feed_grad.astype(jnp.float32), 0)
        feed_rows = gather_grads(feed_grad)
        grad_down = contract(active_low, feed_rows, 0, 0)
        hidden_grad = gelu_pull(contract(feed_rows, down_full, 1, 1))[0].astype(jnp.bfloat16)
        up_total = up_total + jnp.sum(hidden_grad.astype(jnp.float32), 0)
        grad_up = contract(normed_two_rows, hidden_grad, 0, 0)
        normed_two_grad = grads_sum(hidden_grad, up_full, "sc,dc->sd")
        middle_part, gain2_grad, shift2_grad = norm_two_pull(normed_two_grad)
        gain2_total = gain2_total + gain2_grad
        shift2_total = shift2_total + shift2_grad
        middle_grad = grad_stream + middle_part
        branch_grad = middle_grad.astype(jnp.bfloat16)
        out_total = out_total + jnp.sum(branch_grad.astype(jnp.float32), 0)
        branch_rows = gather_grads(branch_grad)
        grad_out = contract(mixed, branch_rows, 0, 0)
        mixed_grad = contract(branch_rows, out_full, 1, 1).astype(jnp.bfloat16).reshape(shape_heads)
        attention = jnp.exp(scores_of(query_heads, key_heads, same_caption) - log_total)
        probs_grad = jnp.einsum(
            "bqhd,bkhd->bhqk", mixed_grad, value_heads, preferred_element_type=jnp.float32
        )
        value_grad = jnp.einsum(
            "bhqk,bqhd->bkhd",
            attention.astype(jnp.bfloat16),
            mixed_grad,
            preferred_element_type=jnp.float32,
        )
        scores_grad = attention * (probs_grad - jnp.sum(attention * probs_grad, -1, keepdims=True))
        scores_grad = scores_grad.astype(jnp.bfloat16)
        query_grad = jnp.einsum(
            "bhqk,bkhd->bqhd", scores_grad, key_heads, preferred_element_type=jnp.float32
        ) * HD ** (-0.5)
        key_grad = jnp.einsum(
            "bhqk,bqhd->bkhd", scores_grad, query_heads, preferred_element_type=jnp.float32
        ) * HD ** (-0.5)
        grad_project = jnp.stack(
            [
                query_grad.reshape(full_rows, head_cols),
                key_grad.reshape(full_rows, head_cols),
                value_grad.reshape(full_rows, head_cols),
            ],
            1,
        ).astype(jnp.bfloat16)
        qv_total = qv_total + jnp.sum(grad_project[:, 0::2].astype(jnp.float32), 0)
        grad_qkv = jnp.einsum(
            "sd,sjc->jdc", normed_rows, grad_project, preferred_element_type=jnp.float32
        )
        normed_grad = grads_sum(grad_project, qkv_full, "sjc,jdc->sd")
        stream_part, gain1_grad, shift1_grad = norm_pull(normed_grad)
        gain1_total = gain1_total + gain1_grad
        shift1_total = shift1_total + shift1_grad
        input_list.append(middle_grad + stream_part)
        full_grads = jax.tree.map(jnp.add, full_grads, (grad_qkv, grad_out, grad_up, grad_down))
    qkv_share, out_share, up_share, down_share = (
        lax.psum_scatter(full_grads[0], "dp", scatter_dimension=1, tiled=True),
        lax.psum_scatter(full_grads[1], "dp", scatter_dimension=1, tiled=True),
        lax.psum_scatter(full_grads[2], "dp", scatter_dimension=0, tiled=True),
        lax.psum_scatter(full_grads[3], "dp", scatter_dimension=1, tiled=True),
    )
    qv_whole = lax.dynamic_update_slice(
        jnp.zeros((2, model_width), jnp.float32), qv_total, (zero_index, tensor_pos * head_cols)
    )
    up_whole = lax.dynamic_update_slice(
        jnp.zeros((hidden_local * lax.axis_size("tensor"),), jnp.float32),
        up_total,
        (tensor_pos * hidden_local,),
    )
    summed = lax.psum(
        (
            qv_whole,
            up_whole,
            out_total,
            down_total,
            gain1_total,
            shift1_total,
            gain2_total,
            shift2_total,
        ),
        ("dp", "tensor"),
    )
    qv_sum, up_sum, out_sum, down_sum, gain1_sum, shift1_sum, gain2_sum, shift2_sum = summed
    return (
        jnp.stack(result_list),
        jnp.stack(input_list),
        gain1_sum,
        shift1_sum,
        qkv_share,
        qv_sum,
        out_share,
        out_sum,
        gain2_sum,
        shift2_sum,
        up_share,
        up_sum,
        down_share,
        down_sum,
    )


def solution(mesh):
    in_specs = (
        P(None, ("dp", "tensor"), None),
        P(None, ("dp", "tensor"), None),
        P(None, "dp", None),
        P(),
        P(),
        P(None, "dp", "tensor"),
        P(None, "tensor"),
        P("tensor", "dp"),
        P(),
        P(),
        P(),
        P("dp", "tensor"),
        P("tensor"),
        P("tensor", "dp"),
        P(),
    )
    out_specs = (
        P(None, ("dp", "tensor"), None),
        P(None, ("dp", "tensor"), None),
        P(),
        P(),
        P(None, "dp", "tensor"),
        P(),
        P("tensor", "dp"),
        P(),
        P(),
        P(),
        P("dp", "tensor"),
        P(),
        P("tensor", "dp"),
        P(),
    )
    return jax.shard_map(body, mesh=mesh, in_specs=in_specs, out_specs=out_specs, check_vma=False)
```

profile of v0, /device:TPU:0, one launch (start us, length us, event | category | flops | bytes accessed | tf_op | source)
XLA Modules:
  0.0 885.6 jit_solution(6010277338871002044)
XLA Ops:
  11.8 21.3 %all_gather.72 = bf16[512,768]{1,0:T(8,128)(2,1)S(1)} all-gather(bf16[128,768]{1,0:T(8,128)(2,1)S(1)} %fusion.157), channel_id=1, replica_groups=mesh['dp'=8,'tensor'=4] {'tensor'}, dimensions={0}, use_global_device_ids=true | all-gather | bytes 983040 | tf_op jit(solution)/shard_map/all_gather | solution.py:31
  33.1 11.5 %all_gather.73 = bf16[3,768,192]{2,1,0:T(8,128)(2,1)S(1)} all-gather(bf16[3,96,192]{2,1,0:T(8,128)(2,1)S(1)} %copy-done.136), channel_id=1, replica_groups=mesh['dp'=8,'tensor'=4] {'dp'}, dimensions={1}, use_global_device_ids=true | all-gather | bytes 995328 | tf_op jit(solution)/shard_map/all_gather | solution.py:111
  46.4 9.2 %all_gather.74 = bf16[192,768]{0,1:T(8,128)(2,1)S(1)} all-gather(bf16[192,96]{0,1:T(8,128)(2,1)S(1)} %copy.47), channel_id=1, replica_groups=mesh['dp'=8,'tensor'=4] {'dp'}, dimensions={1}, use_global_device_ids=true | all-gather | bytes 331776 | tf_op jit(solution)/shard_map/all_gather | solution.py:112
  61.0 21.4 %reduce-scatter.25.cloned.1.call-done = bf16[128,768]{1,0:T(8,128)(2,1)} async-done(((bf16[512,768]{1,0:T(8,128)(2,1)}), bf16[128,768]{1,0:T(8,128)(2,1)}) %reduce-scatter.25.cloned.1.call-update) | async-done | bytes 196624 | tf_op jit(solution)/shard_map/reduce_scatter | solution.py:39
  83.8 17.9 %all_gather.80 = bf16[512,768]{1,0:T(8,128)(2,1)S(1)} all-gather(bf16[128,768]{1,0:T(8,128)(2,1)S(1)} %fusion.153), channel_id=1, replica_groups=mesh['dp'=8,'tensor'=4] {'tensor'}, dimensions={0}, use_global_device_ids=true | all-gather | bytes 983040 | tf_op jit(solution)/shard_map/all_gather | solution.py:31
  110.3 27.7 %all-gather.2 = bf16[1,512,768]{2,1,0:T(8,128)(2,1)} all-gather(bf16[1,128,768]{2,1,0:T(8,128)(2,1)S(1)} %get-tuple-element.151), channel_id=4, replica_groups=mesh['dp'=8,'tensor'=4] {'tensor'}, dimensions={1}, use_global_device_ids=true | all-gather | bytes 983040 | tf_op jit(solution)/shard_map/all_gather | solution.py:35
  137.9 18.3 %all-gather = bf16[1,512,768]{2,1,0:T(8,128)(2,1)} all-gather(bf16[1,128,768]{2,1,0:T(8,128)(2,1)S(1)} %get-tuple-element.149), channel_id=2, replica_groups=mesh['dp'=8,'tensor'=4] {'tensor'}, dimensions={1}, use_global_device_ids=true | all-gather | bytes 983040 | tf_op jit(solution)/shard_map/all_gather | solution.py:35
  163.2 20.1 %all_gather.78 = bf16[512,768]{1,0:T(8,128)(2,1)S(1)} all-gather(bf16[128,768]{1,0:T(8,128)(2,1)S(1)} %get-tuple-element.141), channel_id=1, replica_groups=mesh['dp'=8,'tensor'=4] {'tensor'}, dimensions={0}, use_global_device_ids=true | all-gather | bytes 983040 | tf_op jit(solution)/shard_map/all_gather | solution.py:31
  185.4 15.6 %all_gather.81 = bf16[512,768]{1,0:T(8,128)(2,1)S(1)} all-gather(bf16[128,768]{1,0:T(8,128)(2,1)S(1)} %get-tuple-element.152), channel_id=1, replica_groups=mesh['dp'=8,'tensor'=4] {'tensor'}, dimensions={0}, use_global_device_ids=true | all-gather | bytes 983040 | tf_op jit(solution)/shard_map/all_gather | solution.py:31
  201.0 6.8 multiply_convert_fusion.5
  207.8 4.3 convert_reduce_fusion.1
  214.8 22.9 %all_gather.75 = bf16[512,768]{1,0:T(8,128)(2,1)S(1)} all-gather(bf16[128,768]{1,0:T(8,128)(2,1)S(1)} %copy-done.129), channel_id=1, replica_groups=mesh['dp'=8,'tensor'=4] {'tensor'}, dimensions={0}, use_global_device_ids=true | all-gather | bytes 983040 | tf_op jit(solution)/shard_map/all_gather | solution.py:31
  237.8 6.4 multiply_convert_fusion.7
  244.2 1.8 convert_reduce_fusion.3
  253.8 27.9 %all_gather.82 = bf16[512,768]{1,0:T(8,128)(2,1)S(1)} all-gather(bf16[128,768]{1,0:T(8,128)(2,1)S(1)} %copy-done.128), channel_id=1, replica_groups=mesh['dp'=8,'tensor'=4] {'tensor'}, dimensions={0}, use_global_device_ids=true | all-gather | bytes 983040 | tf_op jit(solution)/shard_map/all_gather | solution.py:31
  289.6 3.3 convolution_convert_fusion.7
  293.1 22.7 %all-gather.3 = bf16[1,512,768]{2,1,0:T(8,128)(2,1)} all-gather(bf16[1,128,768]{2,1,0:T(8,128)(2,1)S(1)} %copy-done.107), channel_id=5, replica_groups=mesh['dp'=8,'tensor'=4] {'tensor'}, dimensions={1}, use_global_device_ids=true | all-gather | bytes 983040 | tf_op jit(solution)/shard_map/all_gather | solution.py:35
  315.8 24.3 %all-gather.1 = bf16[1,512,768]{2,1,0:T(8,128)(2,1)} all-gather(bf16[1,128,768]{2,1,0:T(8,128)(2,1)S(1)} %copy-done.106), channel_id=3, replica_groups=mesh['dp'=8,'tensor'=4] {'tensor'}, dimensions={1}, use_global_device_ids=true | all-gather | bytes 983040 | tf_op jit(solution)/shard_map/all_gather | solution.py:35
  342.6 2.6 fusion.182
  347.5 19.9 %reduce-scatter.27.cloned.1.call-done = bf16[128,768]{1,0:T(8,128)(2,1)} async-done(((bf16[512,768]{1,0:T(8,128)(2,1)}), bf16[128,768]{1,0:T(8,128)(2,1)}) %reduce-scatter.27.cloned.1.call-update) | async-done | bytes 196624 | tf_op jit(solution)/shard_map/reduce_scatter | solution.py:39
  367.5 3.0 fusion.215
  371.4 27.1 %all_gather.83 = bf16[512,768]{1,0:T(8,128)(2,1)S(1)} all-gather(bf16[128,768]{1,0:T(8,128)(2,1)S(1)} %get-tuple-element.137), channel_id=1, replica_groups=mesh['dp'=8,'tensor'=4] {'tensor'}, dimensions={0}, use_global_device_ids=true | all-gather | bytes 983040 | tf_op jit(solution)/shard_map/all_gather | solution.py:31
  398.6 5.2 multiply_convert_fusion.4
  404.4 1.8 convert_reduce_fusion
  408.8 19.2 %all_gather.79 = bf16[512,768]{1,0:T(8,128)(2,1)} all-gather(bf16[128,768]{1,0:T(8,128)(2,1)} %get-tuple-element.136), channel_id=1, replica_groups=mesh['dp'=8,'tensor'=4] {'tensor'}, dimensions={0}, use_global_device_ids=true | all-gather | bytes 983040 | tf_op jit(solution)/shard_map/all_gather | solution.py:31
  428.1 2.1 fusion.217
  430.3 1.8 convert_reduce_fusion.25
  432.1 25.1 %all_gather.89 = bf16[512,768]{1,0:T(8,128)(2,1)S(1)} all-gather(bf16[128,768]{1,0:T(8,128)(2,1)S(1)} %get-tuple-element.109), channel_id=1, replica_groups=mesh['dp'=8,'tensor'=4] {'tensor'}, dimensions={0}, use_global_device_ids=true | all-gather | bytes 983040 | tf_op jit(solution)/shard_map/all_gather | solution.py:35
  459.2 5.2 multiply_convert_fusion.6
  464.5 1.8 convert_reduce_fusion.2
  468.9 2.9 multiply_reduce_fusion.1
  475.6 1.8 bitcast_convert_fusion.1
  477.4 3.2 convolution_convert_fusion.6
  483.4 3.2 convolution_convert_fusion.4
  489.2 2.6 reduce-scatter.45.cloned.1.call-done
  491.7 25.0 %reduce-scatter.51.cloned.1.call-done = bf16[128,768]{1,0:T(8,128)(2,1)} async-done(((bf16[512,768]{1,0:T(8,128)(2,1)}), bf16[128,768]{1,0:T(8,128)(2,1)}) %reduce-scatter.51.cloned.1.call-update) | async-done | bytes 196624 | tf_op jit(solution)/shard_map/reduce_scatter | solution.py:50
  516.7 2.3 fusion.184
  519.6 22.0 %reduce-scatter.31.cloned.1.call-done = bf16[128,768]{1,0:T(8,128)(2,1)} async-done(((bf16[512,768]{1,0:T(8,128)(2,1)}), bf16[128,768]{1,0:T(8,128)(2,1)}) %reduce-scatter.31.cloned.1.call-update) | async-done | bytes 196624 | tf_op jit(solution)/shard_map/reduce_scatter | solution.py:39
  541.6 2.2 fusion.214
  543.8 22.8 %reduce-scatter.39.cloned.1.call-done = bf16[128,768]{1,0:T(8,128)(2,1)} async-done(((bf16[512,768]{1,0:T(8,128)(2,1)}), bf16[128,768]{1,0:T(8,128)(2,1)}) %reduce-scatter.39.cloned.1.call-update) | async-done | bytes 196624 | tf_op jit(solution)/shard_map/reduce_scatter | solution.py:39
  566.6 2.1 fusion.216
  569.6 18.4 %all_gather.85 = bf16[512,768]{1,0:T(8,128)(2,1)S(1)} all-gather(bf16[128,768]{1,0:T(8,128)(2,1)S(1)} %get-tuple-element.145), channel_id=1, replica_groups=mesh['dp'=8,'tensor'=4] {'tensor'}, dimensions={0}, use_global_device_ids=true | all-gather | bytes 983040 | tf_op jit(solution)/shard_map/all_gather | solution.py:35
  592.0 17.4 %all_gather.87 = bf16[512,768]{1,0:T(8,128)(2,1)S(1)} all-gather(bf16[128,768]{1,0:T(8,128)(2,1)S(1)} %get-tuple-element.105), channel_id=1, replica_groups=mesh['dp'=8,'tensor'=4] {'tensor'}, dimensions={0}, use_global_device_ids=true | all-gather | bytes 983040 | tf_op jit(solution)/shard_map/all_gather | solution.py:35
  609.4 17.2 %all_gather.91 = bf16[512,768]{1,0:T(8,128)(2,1)S(1)} all-gather(bf16[128,768]{1,0:T(8,128)(2,1)S(1)} %get-tuple-element.147), channel_id=1, replica_groups=mesh['dp'=8,'tensor'=4] {'tensor'}, dimensions={0}, use_global_device_ids=true | all-gather | bytes 983040 | tf_op jit(solution)/shard_map/all_gather | solution.py:35
  629.1 2.2 copy.82
  633.1 1.9 fusion.48
  636.3 1.7 bitcast_convert_fusion.3
  638.2 2.8 multiply_reduce_fusion.2
  644.4 1.7 bitcast_convert_fusion.2
  646.4 2.8 multiply_reduce_fusion
  654.1 2.0 fusion.81
  658.5 1.9 add_bitcast_fusion
  660.4 4.2 copy.80
  664.6 4.7 reshape.871
  674.6 2.3 add_add_fusion.1
  678.8 2.1 fusion.92
  684.8 2.4 add_add_fusion
  693.4 2.5 pad_maximum_fusion
  698.2 19.8 %reduce-scatter.47.cloned.1.call-done = bf16[128,768]{1,0:T(8,128)(2,1)} async-done(((bf16[512,768]{1,0:T(8,128)(2,1)}), bf16[128,768]{1,0:T(8,128)(2,1)}) %reduce-scatter.47.cloned.1.call-update) | async-done | bytes 196624 | tf_op jit(solution)/shard_map/reduce_scatter | solution.py:50
  718.0 25.0 %reduce-scatter.55.cloned.1.call-done = bf16[128,768]{1,0:T(8,128)(2,1)} async-done(((bf16[512,768]{1,0:T(8,128)(2,1)}), bf16[128,768]{1,0:T(8,128)(2,1)}) %reduce-scatter.55.cloned.1.call-update) | async-done | bytes 196624 | tf_op jit(solution)/shard_map/reduce_scatter | solution.py:50
  743.1 2.3 fusion.183
  749.8 40.9 %all-reduce = (f32[768]{0:T(1024)}, f32[768]{0:T(1024)}, f32[2,768]{1,0:T(2,128)}, f32[768]{0:T(1024)}, f32[768]{0:T(1024)}, /*index=5*/f32[768]{0:T(1024)}, f32[3072]{0:T(1024)}, f32[768]{0:T(1024)}) all-reduce(f32[768]{0:T(1024)} %add_add_fusion.15, f32[768]{0:T(1024)} %add_add_fusion.14, ...), channel_id=1, replica_groups=mesh['dp'=8,'tensor'=4] {'dp','tensor'}, use_global_device_ids=true, to_apply=%region_64.65 | all-reduce | flops 9216 | bytes 73728 | tf_op jit(solution)/shard_map/psum | solution.py:221
  799.0 33.0 %reduce-scatter.57.cloned.1.call-done = f32[96,768]{1,0:T(8,128)} async-done(((f32[768,768]{1,0:T(8,128)}), f32[96,768]{1,0:T(8,128)}) %reduce-scatter.57.cloned.1.call-update) | async-done | bytes 294928 | tf_op jit(solution)/shard_map/reduce_scatter | solution.py:210
  832.0 46.0 %reduce-scatter.59.cloned.1.call-done = f32[768,96]{0,1:T(8,128)} async-done(((f32[768,768]{0,1:T(8,128)}), f32[768,96]{0,1:T(8,128)}) %reduce-scatter.59.cloned.1.call-update) | async-done | bytes 294928 | tf_op jit(solution)/shard_map/reduce_scatter | solution.py:211
  (677 shorter events, 123.0 us)
Async XLA Ops:
  8.0 25.1 %copy-start.136 = (bf16[3,96,192]{2,1,0:T(8,128)(2,1)S(1)}, bf16[3,96,192]{2,1,0:T(8,128)(2,1)}, u32[]{:S(2)}) copy-start(bf16[3,96,192]{2,1,0:T(8,128)(2,1)} %param.20) | copy-start | bytes 331780
  8.0 74.4 %reduce-scatter.25.cloned.1.call-start = ((), (), s32[]{:S(2)}) async-start(), calls=%async_computation.20 | async-start | bytes 983040 | tf_op jit(solution)/shard_map/reduce_scatter | solution.py:39
  9.5 35.2 %copy-start.207 = (f32[2,192]{1,0:T(2,128)S(1)}, f32[2,192]{1,0:T(2,128)}, u32[]{:S(2)}) copy-start(f32[2,192]{1,0:T(2,128)} %param.21) | copy-start | bytes 4612
  9.5 35.6 %copy-start.175 = (f32[128]{0:T(128)}, f32[128]{0:T(128)S(1)}, u32[]{:S(2)}) copy-start(f32[128]{0:T(128)S(1)} %broadcast_multiply_fusion.7) | copy-start | bytes 1540
  10.6 34.5 %copy-start.216 = (f32[128]{0:T(128)}, f32[128]{0:T(128)S(1)}, u32[]{:S(2)}) copy-start(f32[128]{0:T(128)S(1)} %fusion.162) | copy-start | bytes 1540
  10.7 34.4 %copy-start.184 = (f32[128]{0:T(128)}, f32[128]{0:T(128)S(1)}, u32[]{:S(2)}) copy-start(f32[128]{0:T(128)S(1)} %fusion.202) | copy-start | bytes 1540
  44.7 57.4 %copy-start.154 = (f32[1,192]{1,0:T(1,128)}, f32[1,192]{1,0:T(1,128)S(1)}, u32[]{:S(2)}) copy-start(f32[1,192]{1,0:T(1,128)S(1)} %get-tuple-element.158) | copy-start | bytes 2308
  60.8 97.4 %reduce-scatter.33.cloned.1.call-start = ((), (), s32[]{:S(2)}) async-start(), calls=%async_computation.26 | async-start | bytes 983040 | tf_op jit(solution)/shard_map/reduce_scatter | solution.py:39
  60.8 41.3 %copy-start.173 = (f32[128]{0:T(128)}, f32[128]{0:T(128)S(1)}, u32[]{:S(2)}) copy-start(f32[128]{0:T(128)S(1)} %broadcast_multiply_fusion.3) | copy-start | bytes 1540
  108.2 92.9 %all-gather.7.cloned.1.call-start = ((), (), s32[]{:S(2)}) async-start(), calls=%async_computation.21 | async-start | bytes 1327104 | tf_op jit(solution)/shard_map/all_gather | solution.py:113
  108.7 99.1 %all-gather.9.cloned.1.call-start = ((), (), s32[]{:S(2)}) async-start(), calls=%async_computation.22 | async-start | bytes 1327104 | tf_op jit(solution)/shard_map/all_gather | solution.py:114
  109.3 233.2 %reduce-scatter.49.cloned.1.call-start = ((), (), s32[]{:S(2)}) async-start(), calls=%async_computation.34 | async-start | bytes 983040 | tf_op jit(solution)/shard_map/reduce_scatter | solution.py:50
  110.3 47.9 %copy-start.33 = (bf16[128,768]{1,0:T(8,128)(2,1)S(1)}, bf16[128,768]{1,0:T(8,128)(2,1)}, u32[]{:S(2)}) copy-start(bf16[128,768]{1,0:T(8,128)(2,1)} %reduce-scatter.25.cloned.1.call-done) | copy-start | bytes 589828
  183.8 64.8 %copy-start.74 = (bf16[512,192]{0,1:T(8,128)(2,1)}, bf16[512,192]{0,1:T(8,128)(2,1)S(1)}, u32[]{:S(2)}) copy-start(bf16[512,192]{0,1:T(8,128)(2,1)S(1)} %convolution_convert_fusion.18) | copy-start | bytes 589828
  185.4 63.2 %copy-start.62 = (bf16[512,192]{0,1:T(8,128)(2,1)}, bf16[512,192]{0,1:T(8,128)(2,1)S(1)}, u32[]{:S(2)}) copy-start(bf16[512,192]{0,1:T(8,128)(2,1)S(1)} %fusion.59) | copy-start | bytes 589828
  214.8 127.8 %reduce-scatter.41.cloned.1.call-start = ((), (), s32[]{:S(2)}) async-start(), calls=%async_computation.30 | async-start | bytes 983040 | tf_op jit(solution)/shard_map/reduce_scatter | solution.py:50
  248.5 94.0 %reduce-scatter.29.cloned.1.call-start = ((), (), s32[]{:S(2)}) async-start(), calls=%async_computation.24 | async-start | bytes 983040 | tf_op jit(solution)/shard_map/reduce_scatter | solution.py:39
  283.2 59.4 %reduce-scatter.37.cloned.1.call-start = ((), (), s32[]{:S(2)}) async-start(), calls=%async_computation.28 | async-start | bytes 983040 | tf_op jit(solution)/shard_map/reduce_scatter | solution.py:39
  289.6 77.9 %reduce-scatter.27.cloned.1.call-start = ((), (), s32[]{:S(2)}) async-start(), calls=%async_computation.23 | async-start | bytes 983040 | tf_op jit(solution)/shard_map/reduce_scatter | solution.py:39
  293.0 135.1 %reduce-scatter.35.cloned.1.call-start = ((), (), s32[]{:S(2)}) async-start(), calls=%async_computation.27 | async-start | bytes 983040 | tf_op jit(solution)/shard_map/reduce_scatter | solution.py:39
  293.0 47.1 %copy-start.145 = (f32[3,512]{1,0:T(4,128)S(1)}, f32[3,512]{1,0:T(4,128)}, u32[]{:S(2)}) copy-start(f32[3,512]{1,0:T(4,128)} %copy-done.144) | copy-start | bytes 18436
  293.0 47.1 %copy-start.153 = (f32[3,512]{1,0:T(4,128)S(1)}, f32[3,512]{1,0:T(4,128)}, u32[]{:S(2)}) copy-start(f32[3,512]{1,0:T(4,128)} %copy-done.152) | copy-start | bytes 18436
  293.0 47.7 %copy-start.51 = (bf16[512,768]{1,0:T(8,128)(2,1)S(1)}, bf16[512,768]{1,0:T(8,128)(2,1)}, u32[]{:S(2)}) copy-start(bf16[512,768]{1,0:T(8,128)(2,1)} %get-tuple-element.124) | copy-start | bytes 2359300
  293.0 47.7 %copy-start.228 = (bf16[768,768]{0,1:T(8,128)(2,1)S(1)}, bf16[768,768]{0,1:T(8,128)(2,1)}, u32[]{:S(2)}) copy-start(bf16[768,768]{0,1:T(8,128)(2,1)} %all-gather.9.cloned.1.call-done) | copy-start | bytes 3538948
  342.4 25.0 %copy-start.146 = (f32[768]{0:T(1024)S(1)}, f32[768]{0:T(1024)}, u32[]{:S(2)}) copy-start(f32[768]{0:T(1024)} %param.29) | copy-start | bytes 9220
  342.5 146.7 %reduce-scatter.53.cloned.1.call-start = ((), (), s32[]{:S(2)}) async-start(), calls=%async_computation.36 | async-start | bytes 983040 | tf_op jit(solution)/shard_map/reduce_scatter | solution.py:50
  370.5 28.1 %copy-start.233 = (bf16[768,768]{1,0:T(8,128)(2,1)S(1)}, bf16[768,768]{1,0:T(8,128)(2,1)}, u32[]{:S(2)}) copy-start(bf16[768,768]{1,0:T(8,128)(2,1)} %all-gather.7.cloned.1.call-done) | copy-start | bytes 3538948
  370.5 28.1 %copy-start.236 = (f32[768]{0:T(1024)S(1)}, f32[768]{0:T(1024)}, u32[]{:S(2)}) copy-start(f32[768]{0:T(1024)} %param.27) | copy-start | bytes 9220
  428.0 63.7 %reduce-scatter.45.cloned.1.call-start = ((), (), s32[]{:S(2)}) async-start(), calls=%async_computation.32 | async-start | bytes 983040 | tf_op jit(solution)/shard_map/reduce_scatter | solution.py:50
  430.2 29.0 %copy-start.28 = (bf16[512,768]{1,0:T(8,128)(2,1)S(1)}, bf16[512,768]{1,0:T(8,128)(2,1)}, u32[]{:S(2)}) copy-start(bf16[512,768]{1,0:T(8,128)(2,1)} %all_gather.79) | copy-start | bytes 2359300
  430.3 29.0 %copy-start.234 = (bf16[768,768]{1,0:T(8,128)(2,1)S(1)}, bf16[768,768]{1,0:T(8,128)(2,1)}, u32[]{:S(2)}) copy-start(bf16[768,768]{1,0:T(8,128)(2,1)} %all-gather.7.cloned.1.call-done) | copy-start | bytes 3538948
  430.3 29.0 %copy-start.237 = (f32[768]{0:T(1024)S(1)}, f32[768]{0:T(1024)}, u32[]{:S(2)}) copy-start(f32[768]{0:T(1024)} %param.27) | copy-start | bytes 9220
  468.9 47.9 %reduce-scatter.51.cloned.1.call-start = ((), (), s32[]{:S(2)}) async-start(), calls=%async_computation.35 | async-start | bytes 983040 | tf_op jit(solution)/shard_map/reduce_scatter | solution.py:50
  477.4 64.3 %reduce-scatter.31.cloned.1.call-start = ((), (), s32[]{:S(2)}) async-start(), calls=%async_computation.25 | async-start | bytes 983040 | tf_op jit(solution)/shard_map/reduce_scatter | solution.py:39
  480.7 85.9 %reduce-scatter.39.cloned.1.call-start = ((), (), s32[]{:S(2)}) async-start(), calls=%async_computation.29 | async-start | bytes 983040 | tf_op jit(solution)/shard_map/reduce_scatter | solution.py:39
  486.6 210.0 %reduce-scatter.63.cloned.1.call-start = ((), (), s32[]{:S(2)}) async-start(), calls=%async_computation.41 | async-start | bytes 884736
  543.8 25.9 %copy-start.199 = (f32[128]{0:T(128)}, f32[128]{0:T(128)S(1)}, u32[]{:S(2)}) copy-start(f32[128]{0:T(128)S(1)} %negate_multiply_fusion.9) | copy-start | bytes 1540
  590.7 35.9 %copy-start.10 = (bf16[3,512,512]{1,2,0:T(8,128)(2,1)}, bf16[3,512,512]{1,2,0:T(8,128)(2,1)S(1)}, u32[]{:S(2)}) copy-start(bf16[3,512,512]{1,2,0:T(8,128)(2,1)S(1)} %multiply_convert_fusion.3) | copy-start | bytes 4718596
  590.7 35.9 %copy-start.103 = (bf16[3,64,512]{2,1,0:T(8,128)(2,1)S(1)}, bf16[3,64,512]{2,1,0:T(8,128)(2,1)}, u32[]{:S(2)}) copy-start(bf16[3,64,512]{2,1,0:T(8,128)(2,1)} %copy-done.102) | copy-start | bytes 589828
  631.3 66.9 %reduce-scatter.43.cloned.1.call-start = ((), (), s32[]{:S(2)}) async-start(), calls=%async_computation.31 | async-start | bytes 983040 | tf_op jit(solution)/shard_map/reduce_scatter | solution.py:50
  638.1 80.0 %reduce-scatter.47.cloned.1.call-start = ((), (), s32[]{:S(2)}) async-start(), calls=%async_computation.33 | async-start | bytes 983040 | tf_op jit(solution)/shard_map/reduce_scatter | solution.py:50
  646.1 96.9 %reduce-scatter.55.cloned.1.call-start = ((), (), s32[]{:S(2)}) async-start(), calls=%async_computation.37 | async-start | bytes 983040 | tf_op jit(solution)/shard_map/reduce_scatter | solution.py:50
  654.0 143.1 %reduce-scatter.61.cloned.1.call-start = ((), (), s32[]{:S(2)}) async-start(), calls=%async_computation.40 | async-start | bytes 2211840
  669.3 162.7 %reduce-scatter.57.cloned.1.call-start = ((), (), s32[]{:S(2)}) async-start(), calls=%async_computation.38 | async-start | bytes 2654208 | tf_op jit(solution)/shard_map/reduce_scatter | solution.py:210
  676.9 201.1 %reduce-scatter.59.cloned.1.call-start = ((), (), s32[]{:S(2)}) async-start(), calls=%async_computation.39 | async-start | bytes 2654208 | tf_op jit(solution)/shard_map/reduce_scatter | solution.py:211
  693.4 49.7 %copy-start.55 = (bf16[128,768]{1,0:T(8,128)(2,1)S(1)}, bf16[128,768]{1,0:T(8,128)(2,1)}, u32[]{:S(2)}) copy-start(bf16[128,768]{1,0:T(8,128)(2,1)} %reduce-scatter.51.cloned.1.call-done) | copy-start | bytes 589828
  693.4 49.7 %copy-start.157 = (f32[128]{0:T(128)S(1)}, f32[128]{0:T(128)}, u32[]{:S(2)}) copy-start(f32[128]{0:T(128)} %copy-done.156) | copy-start | bytes 1540
  693.4 49.7 %copy-start.159 = (f32[128]{0:T(128)S(1)}, f32[128]{0:T(128)}, u32[]{:S(2)}) copy-start(f32[128]{0:T(128)} %copy-done.158) | copy-start | bytes 1540
  693.4 49.7 %copy-start.174 = (f32[128]{0:T(128)S(1)}, f32[128]{0:T(128)}, u32[]{:S(2)}) copy-start(f32[128]{0:T(128)} %copy-done.173) | copy-start | bytes 1540
  693.4 49.7 %copy-start.176 = (f32[128]{0:T(128)S(1)}, f32[128]{0:T(128)}, u32[]{:S(2)}) copy-start(f32[128]{0:T(128)} %copy-done.175) | copy-start | bytes 1540
  693.4 49.7 %copy-start.187 = (f32[128]{0:T(128)S(1)}, f32[128]{0:T(128)}, u32[]{:S(2)}) copy-start(f32[128]{0:T(128)} %copy-done.186) | copy-start | bytes 1540
  693.4 49.7 %copy-start.201 = (f32[128]{0:T(128)S(1)}, f32[128]{0:T(128)}, u32[]{:S(2)}) copy-start(f32[128]{0:T(128)} %multiply_multiply_fusion.22) | copy-start | bytes 1540
  695.9 49.5 %copy-start.212 = (f32[128]{0:T(128)S(1)}, f32[128]{0:T(128)}, u32[]{:S(2)}) copy-start(f32[128]{0:T(128)} %copy-done.211) | copy-start | bytes 1540
  695.9 49.6 %copy-start.210 = (f32[128]{0:T(128)S(1)}, f32[128]{0:T(128)}, u32[]{:S(2)}) copy-start(f32[128]{0:T(128)} %copy-done.209) | copy-start | bytes 1540
  695.9 49.6 %copy-start.217 = (f32[128]{0:T(128)S(1)}, f32[128]{0:T(128)}, u32[]{:S(2)}) copy-start(f32[128]{0:T(128)} %copy-done.216) | copy-start | bytes 1540
  695.9 50.7 %copy-start.185 = (f32[128]{0:T(128)S(1)}, f32[128]{0:T(128)}, u32[]{:S(2)}) copy-start(f32[128]{0:T(128)} %copy-done.184) | copy-start | bytes 1540
  695.9 50.7 %copy-start.189 = (f32[128]{0:T(128)S(1)}, f32[128]{0:T(128)}, u32[]{:S(2)}) copy-start(f32[128]{0:T(128)} %copy-done.188) | copy-start | bytes 1540
  695.9 50.7 %copy-start.191 = (f32[128]{0:T(128)S(1)}, f32[128]{0:T(128)}, u32[]{:S(2)}) copy-start(f32[128]{0:T(128)} %copy-done.190) | copy-start | bytes 1540
  696.0 97.3 %copy-start.39 = (f32[128,768]{1,0:T(8,128)S(1)}, f32[128,768]{1,0:T(8,128)}, u32[]{:S(2)}) copy-start(f32[128,768]{1,0:T(8,128)} %copy-done.38) | copy-start | bytes 1179652
  696.0 97.3 %copy-start.41 = (f32[128,768]{1,0:T(8,128)S(1)}, f32[128,768]{1,0:T(8,128)}, u32[]{:S(2)}) copy-start(f32[128,768]{1,0:T(8,128)} %copy-done.40) | copy-start | bytes 1179652
  698.2 48.4 %copy-start.56 = (bf16[128,768]{1,0:T(8,128)(2,1)S(1)}, bf16[128,768]{1,0:T(8,128)(2,1)}, u32[]{:S(2)}) copy-start(bf16[128,768]{1,0:T(8,128)(2,1)} %reduce-scatter.43.cloned.1.call-done) | copy-start | bytes 589828
  718.0 28.6 %copy-start.57 = (bf16[128,768]{1,0:T(8,128)(2,1)S(1)}, bf16[128,768]{1,0:T(8,128)(2,1)}, u32[]{:S(2)}) copy-start(bf16[128,768]{1,0:T(8,128)(2,1)} %reduce-scatter.47.cloned.1.call-done) | copy-start | bytes 589828
  747.9 46.7 %copy-start.35 = (f32[128,768]{1,0:T(8,128)S(1)}, f32[128,768]{1,0:T(8,128)}, u32[]{:S(2)}) copy-start(f32[128,768]{1,0:T(8,128)} %get-tuple-element.115) | copy-start | bytes 1179652
  747.9 46.7 %copy-start.37 = (f32[128,768]{1,0:T(8,128)S(1)}, f32[128,768]{1,0:T(8,128)}, u32[]{:S(2)}) copy-start(f32[128,768]{1,0:T(8,128)} %get-tuple-element.113) | copy-start | bytes 1179652
  (196 other events, 944.4 us)
Sparse Core Ops, SparseCore 0:
  60.9 21.5 reduce-scatter.24
  108.3 31.8 reduce-scatter.32
  214.9 30.3 reduce-scatter.48
  248.7 32.4 reduce-scatter.40
  283.4 29.5 reduce-scatter.28
  315.1 26.2 reduce-scatter.36
  343.7 23.7 reduce-scatter.26
  369.7 31.7 reduce-scatter.34
  428.2 29.1 reduce-scatter.52
  469.0 22.6 reduce-scatter.44
  494.0 22.6 reduce-scatter.50
  518.9 22.6 reduce-scatter.30
  543.9 22.6 reduce-scatter.38
Sparse Core Ops, SparseCore 1:
  110.5 23.2 all-gather.6
  135.6 23.8 all-gather.8
  631.4 35.4 reduce-scatter.62
  669.7 23.2 reduce-scatter.42
  695.4 22.6 reduce-scatter.46
  720.4 22.7 reduce-scatter.54
  746.3 39.5 reduce-scatter.60
  789.7 42.2 reduce-scatter.56
  835.8 42.2 reduce-scatter.58
where the time goes:
time: 895 us; the launch traced here: 886 us
  blocking collectives  405 us (45%)
  waiting for transfers between devices  239 us (27%)
  matrix products  116 us (13%)
  other arithmetic  64 us (7%)
  local copies, waits for them, and re-layouts  41 us (5%)
  between operations  18.4 us (2%)
    all_gather x8, blocking collectives, gather_rows(): return lax.all_gather(values_low, 'tensor', axis=0, tiled=True)  172 us
    all_gather x8, blocking collectives, gather_grads(): return lax.all_gather(values_low, 'tensor', axis=0, tiled=True)  171 us
    reduce_scatter x8, waiting for transfers between devices, rows_sum(): lax.psum_scatter(jnp.einsum(einsum_form, operand_left, operand_right, pre...  86.2 us
    reduce_scatter x8, waiting for transfers between devices, grads_sum(): lax.psum_scatter(jnp.einsum(einsum_form, operand_left, operand_right, pre...  72.5 us
    dot_general x36, matrix products, contract(): lax.dot_general(operand_left, operand_right, (((left_dim,), (right_dim,))...  56.3 us
    reduce_scatter x1, waiting for transfers between devices, body(): lax.psum_scatter(full_grads[3], 'dp', scatter_dimension=1, tiled=True)  46 us
    psum x1, blocking collectives, body(): lax.psum((qv_whole, up_whole, out_total, down_total, gain1_total, shift1_...  40.9 us
    unnamed x483, local copies, waits for them, and re-layouts  39.4 us
  transfers between devices with their start and end apart: 22, of which 10 were waited for; matrix products, arithmetic and copies ran while one was open for 19% of the time, Pallas kernels for 0%

commit v1 on v0

--- a/solution.py
+++ b/solution.py
@@ -1,3 +1,4 @@
+import functools
 import jax
 import jax.numpy as jnp
 from jax import lax
@@ -6,6 +7,31 @@
 HD = 64
 epsilon = 1e-05
 masked_value = -1000000000.0
+
+
+def state_spots(inner_x, join_dim):
+    y1 = list(inner_x.shape[1:])
+    y1[join_dim] *= inner_x.shape[0]
+    return jnp.moveaxis(inner_x, 0, join_dim).reshape(y1)
+
+
+def answer_the_windows(xx, net_axis, dim_k):
+    workers = lax.axis_size(net_axis)
+    windows = tuple(((p, (p + 1) % workers) for p in range(workers)))
+    heap = tuple(((h, at) for at, h in windows))
+    field_out, s_next = ([], [])
+    for q in range(workers - 1):
+        if q % 2 == 0:
+            field_out.append(lax.ppermute(field_out[-1] if field_out else xx, net_axis, windows))
+        else:
+            s_next.append(lax.ppermute(s_next[-1] if s_next else xx, net_axis, heap))
+    y2 = jnp.stack([*field_out[::-1], xx, *s_next], axis=0)
+    t_next = lax.axis_index(net_axis) - len(field_out)
+    y2 = y2[(jnp.arange(workers) - t_next) % workers]
+    return state_spots(y2, dim_k)
+
+
+follow_steps_all = functools.partial(answer_the_windows, net_axis="tensor", dim_k=0)
 
 
 def layer_norm(stream_values, scales, shifts):
@@ -28,7 +54,7 @@
 
 
 def gather_rows(values_low):
-    return lax.all_gather(values_low, "tensor", axis=0, tiled=True)
+    return follow_steps_all(values_low)
 
 
 def gather_grads(values_low):

time: 895 us -> 864 us (0.965)
  blocking collectives: 405 us -> 222 us
  waiting for transfers between devices: 239 us -> 329 us
  starting transfers between devices: 1.49 us -> 30.2 us
  other arithmetic: 64 us -> 79.6 us
  local copies, waits for them, and re-layouts: 41 us -> 56.1 us
    all_gather x8 -> x0, blocking collectives: 172 us -> none  [gather_rows(): return lax.all_gather(values_low, 'tensor', axis=0, tiled=True)]
    ppermute x0 -> x24, waiting for transfers between devices: none -> 50.2 us  [the longest x16 44.9 us: answer_the_windows(): lax.ppermute(field_out[-1] if field_out else xx, net_axis, windows)]
    reduce_scatter x8, waiting for transfers between devices: 86.2 us -> 127 us  [rows_sum(): lax.psum_scatter(jnp.einsum(einsum_form, operand_left, operand_right, pre...]
    ppermute x0 -> x24, starting transfers between devices: none -> 27.9 us  [the longest x8 22.1 us: answer_the_windows(): s_next.append(lax.ppermute(s_next[-1] if s_next else xx, net_axis, heap))]
    gather x0 -> x8, local copies, waits for them, and re-layouts: none -> 16.3 us  [answer_the_windows(): y2 = y2[(jnp.arange(workers) - t_next) % workers]]
    another operation x0 -> x8, other arithmetic: none -> 12.8 us  [answer_the_windows(): y2 = jnp.stack([*field_out[::-1], xx, *s_next], axis=0)]
    all_gather x8, blocking collectives: 171 us -> 160 us  [gather_grads(): return lax.all_gather(values_low, 'tensor', axis=0, tiled=True)]
  transfers between devices with their start and end apart: 22 -> 46, of which waited for: 10 -> 21; matrix products, arithmetic and copies ran while one was open for 19% -> 24% of each run, Pallas kernels for 0% -> 0%
where the time goes in v1:
time: 864 us; the launch traced here: 853 us
  waiting for transfers between devices  329 us (38%)
  blocking collectives  222 us (26%)
  matrix products  117 us (14%)
  other arithmetic  79.6 us (9%)
  local copies, waits for them, and re-layouts  56.1 us (6%)
  starting transfers between devices  30.2 us (3%)
  between operations  18.6 us (2%)
    all_gather x8, blocking collectives, gather_grads(): return lax.all_gather(values_low, 'tensor', axis=0, tiled=True)  160 us
    reduce_scatter x8, waiting for transfers between devices, rows_sum(): lax.psum_scatter(jnp.einsum(einsum_form, operand_left, operand_right, pre...  127 us
    reduce_scatter x8, waiting for transfers between devices, grads_sum(): lax.psum_scatter(jnp.einsum(einsum_form, operand_left, operand_right, pre...  71.5 us
    dot_general x36, matrix products, contract(): lax.dot_general(operand_left, operand_right, (((left_dim,), (right_dim,))...  57.3 us
    reduce_scatter x1, waiting for transfers between devices, body(): lax.psum_scatter(full_grads[3], 'dp', scatter_dimension=1, tiled=True)  46 us
    ppermute x16, waiting for transfers between devices, answer_the_windows(): lax.ppermute(field_out[-1] if field_out else xx, net_axis, windows)  44.9 us
    psum x1, blocking collectives, body(): lax.psum((qv_whole, up_whole, out_total, down_total, gain1_total, shift1_...  41 us
    unnamed x483, local copies, waits for them, and re-layouts  38.2 us
  transfers between devices with their start and end apart: 46, of which 21 were waited for; matrix products, arithmetic and copies ran while one was open for 24% of the time, Pallas kernels for 0%

profile of v1, /device:TPU:0, one launch (start us, length us, event | category | flops | bytes accessed | tf_op | source)
XLA Modules:
  0.0 853.0 jit_solution(8556266020117065071)
XLA Ops:
  11.8 5.1 collective-permute-start.2
  18.6 7.7 collective-permute-done
  27.9 9.6 %all_gather.49 = bf16[192,768]{0,1:T(8,128)(2,1)S(1)} all-gather(bf16[192,96]{0,1:T(8,128)(2,1)S(1)} %copy.47), channel_id=1, replica_groups=mesh['dp'=8,'tensor'=4] {'dp'}, dimensions={1}, use_global_device_ids=true | all-gather | bytes 331776 | tf_op jit(solution)/shard_map/all_gather | solution.py:138
  37.4 11.7 %all_gather.48 = bf16[3,768,192]{2,1,0:T(8,128)(2,1)S(1)} all-gather(bf16[3,96,192]{2,1,0:T(8,128)(2,1)S(1)} %copy-done.133), channel_id=1, replica_groups=mesh['dp'=8,'tensor'=4] {'dp'}, dimensions={1}, use_global_device_ids=true | all-gather | bytes 995328 | tf_op jit(solution)/shard_map/all_gather | solution.py:137
  56.4 22.1 %reduce-scatter.25.cloned.1.call-done = bf16[128,768]{1,0:T(8,128)(2,1)} async-done(((bf16[512,768]{1,0:T(8,128)(2,1)}), bf16[128,768]{1,0:T(8,128)(2,1)}) %reduce-scatter.25.cloned.1.call-update) | async-done | bytes 196624 | tf_op jit(solution)/shard_map/reduce_scatter | solution.py:65
  80.1 3.9 collective-permute-start.14
  84.0 5.5 collective-permute-done.12
  90.5 6.5 collective-permute-done.13
  108.3 27.9 %all-gather.2 = bf16[1,512,768]{2,1,0:T(8,128)(2,1)} all-gather(bf16[1,128,768]{2,1,0:T(8,128)(2,1)S(1)} %get-tuple-element.153), channel_id=4, replica_groups=mesh['dp'=8,'tensor'=4] {'tensor'}, dimensions={1}, use_global_device_ids=true | all-gather | bytes 983040 | tf_op jit(solution)/shard_map/all_gather | solution.py:61
  136.3 17.2 %all-gather = bf16[1,512,768]{2,1,0:T(8,128)(2,1)} all-gather(bf16[1,128,768]{2,1,0:T(8,128)(2,1)S(1)} %get-tuple-element.151), channel_id=2, replica_groups=mesh['dp'=8,'tensor'=4] {'tensor'}, dimensions={1}, use_global_device_ids=true | all-gather | bytes 983040 | tf_op jit(solution)/shard_map/all_gather | solution.py:61
  160.9 3.6 collective-permute-start.17
  166.6 2.8 collective-permute-done.15
  171.0 4.5 collective-permute-done.17
  175.5 10.7 %collective-permute-done.6 = bf16[128,768]{1,0:T(8,128)(2,1)S(1)} collective-permute-done((bf16[128,768]{1,0:T(8,128)(2,1)}, bf16[128,768]{1,0:T(8,128)(2,1)S(1)}, u32[]{:S(2)}, u32[]{:S(2)}) %collective-permute-start.6) | collective-permute-done | bytes 196640 | tf_op jit(solution)/shard_map/ppermute | solution.py:25
  191.6 6.8 multiply_convert_fusion.5
  198.4 4.3 convert_reduce_fusion.1
  204.5 3.4 collective-permute-start.20
  212.8 4.6 collective-permute-done.4
  217.4 2.2 pad_maximum_fusion.3
  219.6 2.8 gather_fusion.1
  222.4 6.4 multiply_convert_fusion.7
  241.4 2.6 fusion.66
  254.3 3.2 convolution_convert_fusion.7
  257.7 24.4 %all-gather.3 = bf16[1,512,768]{2,1,0:T(8,128)(2,1)} all-gather(bf16[1,128,768]{2,1,0:T(8,128)(2,1)S(1)} %copy-done.105), channel_id=5, replica_groups=mesh['dp'=8,'tensor'=4] {'tensor'}, dimensions={1}, use_global_device_ids=true | all-gather | bytes 983040 | tf_op jit(solution)/shard_map/all_gather | solution.py:61
  282.1 19.5 %all-gather.1 = bf16[1,512,768]{2,1,0:T(8,128)(2,1)} all-gather(bf16[1,128,768]{2,1,0:T(8,128)(2,1)S(1)} %copy-done.104), channel_id=3, replica_groups=mesh['dp'=8,'tensor'=4] {'tensor'}, dimensions={1}, use_global_device_ids=true | all-gather | bytes 983040 | tf_op jit(solution)/shard_map/all_gather | solution.py:61
  304.2 14.1 %reduce-scatter.37.cloned.1.call-done = bf16[128,768]{1,0:T(8,128)(2,1)} async-done(((bf16[512,768]{1,0:T(8,128)(2,1)}), bf16[128,768]{1,0:T(8,128)(2,1)}) %reduce-scatter.37.cloned.1.call-update) | async-done | bytes 196624 | tf_op jit(solution)/shard_map/reduce_scatter | solution.py:65
  318.2 2.6 fusion.191
  323.0 20.3 %reduce-scatter.27.cloned.1.call-done = bf16[128,768]{1,0:T(8,128)(2,1)} async-done(((bf16[512,768]{1,0:T(8,128)(2,1)}), bf16[128,768]{1,0:T(8,128)(2,1)}) %reduce-scatter.27.cloned.1.call-update) | async-done | bytes 196624 | tf_op jit(solution)/shard_map/reduce_scatter | solution.py:65
  343.3 3.0 fusion.229
  349.4 3.7 collective-permute-start.11
  353.6 25.7 %reduce-scatter.35.cloned.1.call-done = bf16[128,768]{1,0:T(8,128)(2,1)} async-done(((bf16[512,768]{1,0:T(8,128)(2,1)}), bf16[128,768]{1,0:T(8,128)(2,1)}) %reduce-scatter.35.cloned.1.call-update) | async-done | bytes 196624 | tf_op jit(solution)/shard_map/reduce_scatter | solution.py:65
  379.4 2.1 fusion.231
  383.4 18.3 %all_gather.57 = bf16[512,768]{1,0:T(8,128)(2,1)S(1)} all-gather(bf16[128,768]{1,0:T(8,128)(2,1)S(1)} %get-tuple-element.109), channel_id=1, replica_groups=mesh['dp'=8,'tensor'=4] {'tensor'}, dimensions={0}, use_global_device_ids=true | all-gather | bytes 983040 | tf_op jit(solution)/shard_map/all_gather | solution.py:61
  410.3 5.0 collective-permute-done.22
  415.3 2.2 pad_maximum_fusion.9
  417.5 2.8 gather_fusion.7
  420.3 2.2 pad_maximum_fusion.5
  422.5 2.8 gather_fusion.3
  425.3 6.4 multiply_convert_fusion.4
  436.3 6.4 multiply_convert_fusion.6
  447.4 3.2 convolution_convert_fusion.6
  453.4 3.3 convolution_convert_fusion.4
  459.3 25.0 %reduce-scatter.45.cloned.1.call-done = bf16[128,768]{1,0:T(8,128)(2,1)} async-done(((bf16[512,768]{1,0:T(8,128)(2,1)}), bf16[128,768]{1,0:T(8,128)(2,1)}) %reduce-scatter.45.cloned.1.call-update) | async-done | bytes 196624 | tf_op jit(solution)/shard_map/reduce_scatter | solution.py:76
  484.3 2.3 fusion.193
  487.1 22.0 %reduce-scatter.31.cloned.1.call-done = bf16[128,768]{1,0:T(8,128)(2,1)} async-done(((bf16[512,768]{1,0:T(8,128)(2,1)}), bf16[128,768]{1,0:T(8,128)(2,1)}) %reduce-scatter.31.cloned.1.call-update) | async-done | bytes 196624 | tf_op jit(solution)/shard_map/reduce_scatter | solution.py:65
  509.1 2.1 fusion.228
  511.3 22.8 %reduce-scatter.39.cloned.1.call-done = bf16[128,768]{1,0:T(8,128)(2,1)} async-done(((bf16[512,768]{1,0:T(8,128)(2,1)}), bf16[128,768]{1,0:T(8,128)(2,1)}) %reduce-scatter.39.cloned.1.call-update) | async-done | bytes 196624 | tf_op jit(solution)/shard_map/reduce_scatter | solution.py:65
  537.2 18.0 %all_gather.53 = bf16[512,768]{1,0:T(8,128)(2,1)S(1)} all-gather(bf16[128,768]{1,0:T(8,128)(2,1)S(1)} %get-tuple-element.147), channel_id=1, replica_groups=mesh['dp'=8,'tensor'=4] {'tensor'}, dimensions={0}, use_global_device_ids=true | all-gather | bytes 983040 | tf_op jit(solution)/shard_map/all_gather | solution.py:61
  559.1 17.5 %all_gather.55 = bf16[512,768]{1,0:T(8,128)(2,1)S(1)} all-gather(bf16[128,768]{1,0:T(8,128)(2,1)S(1)} %get-tuple-element.105), channel_id=1, replica_groups=mesh['dp'=8,'tensor'=4] {'tensor'}, dimensions={0}, use_global_device_ids=true | all-gather | bytes 983040 | tf_op jit(solution)/shard_map/all_gather | solution.py:61
  576.6 17.1 %all_gather.59 = bf16[512,768]{1,0:T(8,128)(2,1)S(1)} all-gather(bf16[128,768]{1,0:T(8,128)(2,1)S(1)} %get-tuple-element.149), channel_id=1, replica_groups=mesh['dp'=8,'tensor'=4] {'tensor'}, dimensions={0}, use_global_device_ids=true | all-gather | bytes 983040 | tf_op jit(solution)/shard_map/all_gather | solution.py:61
  596.2 2.2 copy.82
  605.8 2.8 multiply_reduce_fusion.2
  613.8 2.8 multiply_reduce_fusion
  627.3 4.2 copy.80
  631.6 4.6 reshape.1112
  641.5 2.3 add_add_fusion.1
  650.8 2.4 add_add_fusion
  659.4 2.5 pad_maximum_fusion
  664.2 21.5 %reduce-scatter.47.cloned.1.call-done = bf16[128,768]{1,0:T(8,128)(2,1)} async-done(((bf16[512,768]{1,0:T(8,128)(2,1)}), bf16[128,768]{1,0:T(8,128)(2,1)}) %reduce-scatter.47.cloned.1.call-update) | async-done | bytes 196624 | tf_op jit(solution)/shard_map/reduce_scatter | solution.py:76
  685.6 25.0 %reduce-scatter.55.cloned.1.call-done = bf16[128,768]{1,0:T(8,128)(2,1)} async-done(((bf16[512,768]{1,0:T(8,128)(2,1)}), bf16[128,768]{1,0:T(8,128)(2,1)}) %reduce-scatter.55.cloned.1.call-update) | async-done | bytes 196624 | tf_op jit(solution)/shard_map/reduce_scatter | solution.py:76
  710.7 2.3 fusion.192
  717.4 41.0 %all-reduce = (f32[768]{0:T(1024)}, f32[768]{0:T(1024)}, f32[2,768]{1,0:T(2,128)}, f32[768]{0:T(1024)}, f32[768]{0:T(1024)}, /*index=5*/f32[768]{0:T(1024)}, f32[3072]{0:T(1024)}, f32[768]{0:T(1024)}) all-reduce(f32[768]{0:T(1024)} %add_add_fusion.15, f32[768]{0:T(1024)} %add_add_fusion.14, ...), channel_id=1, replica_groups=mesh['dp'=8,'tensor'=4] {'dp','tensor'}, use_global_device_ids=true, to_apply=%region_64.65 | all-reduce | flops 9216 | bytes 73728 | tf_op jit(solution)/shard_map/psum | solution.py:247
  766.6 32.8 %reduce-scatter.57.cloned.1.call-done = f32[96,768]{1,0:T(8,128)} async-done(((f32[768,768]{1,0:T(8,128)}), f32[96,768]{1,0:T(8,128)}) %reduce-scatter.57.cloned.1.call-update) | async-done | bytes 294928 | tf_op jit(solution)/shard_map/reduce_scatter | solution.py:236
  799.4 46.0 %reduce-scatter.59.cloned.1.call-done = f32[768,96]{0,1:T(8,128)} async-done(((f32[768,768]{0,1:T(8,128)}), f32[768,96]{0,1:T(8,128)}) %reduce-scatter.59.cloned.1.call-update) | async-done | bytes 294928 | tf_op jit(solution)/shard_map/reduce_scatter | solution.py:237
  (738 shorter events, 171.8 us)
Async XLA Ops:
  8.1 70.5 %reduce-scatter.25.cloned.1.call-start = ((), (), s32[]{:S(2)}) async-start(), calls=%async_computation.20 | async-start | bytes 983040 | tf_op jit(solution)/shard_map/reduce_scatter | solution.py:65
  11.8 37.3 %collective-permute-start.2 = (bf16[128,768]{1,0:T(8,128)(2,1)S(1)}, bf16[128,768]{1,0:T(8,128)(2,1)S(1)}, u32[]{:S(2)}, u32[]{:S(2)}) collective-permute-start(bf16[128,768]{1,0:T(8,128)(2,1)S(1)} %fusion.144), channel_id=1, source_target_pairs={{1,0},{2,1},{3,2},{0,3},{5,4},{6,5},{7,6},{4,7},{9,8},{10,9},{11,1... | collective-permute-start | bytes 589832 | tf_op jit(solution)/shard_map/ppermute | solution.py:27
  17.0 9.3 %collective-permute-start = (bf16[128,768]{1,0:T(8,128)(2,1)S(1)}, bf16[128,768]{1,0:T(8,128)(2,1)S(1)}, u32[]{:S(2)}, u32[]{:S(2)}) collective-permute-start(bf16[128,768]{1,0:T(8,128)(2,1)S(1)} %fusion.144), channel_id=1, source_target_pairs={{0,1},{1,2},{2,3},{3,0},{4,5},{5,6},{6,7},{7,4},{8,9},{9,10},{10,1... | collective-permute-start | bytes 589832 | tf_op jit(solution)/shard_map/ppermute | solution.py:25
  18.2 79.8 %copy-start.177 = (s32[1024]{0:T(1024)}, s32[1024]{0:T(1024)S(1)}, u32[]{:S(2)}) copy-start(s32[1024]{0:T(1024)S(1)} %pad_clamp_fusion) | copy-start | bytes 12292
  18.6 81.1 %copy-start.151 = (f32[1,192]{1,0:T(1,128)}, f32[1,192]{1,0:T(1,128)S(1)}, u32[]{:S(2)}) copy-start(f32[1,192]{1,0:T(1,128)S(1)} %get-tuple-element.161) | copy-start | bytes 2308
  18.6 81.6 %copy-start.153 = (f32[1,192]{1,0:T(1,128)}, f32[1,192]{1,0:T(1,128)S(1)}, u32[]{:S(2)}) copy-start(f32[1,192]{1,0:T(1,128)S(1)} %get-tuple-element.160) | copy-start | bytes 2308
  26.2 22.9 %collective-permute-start.1 = (bf16[128,768]{1,0:T(8,128)(2,1)S(1)}, bf16[128,768]{1,0:T(8,128)(2,1)S(1)}, u32[]{:S(2)}, u32[]{:S(2)}) collective-permute-start(bf16[128,768]{1,0:T(8,128)(2,1)S(1)} %collective-permute-done), channel_id=1, source_target_pairs={{0,1},{1,2},{2,3},{3,0},{4,5},{5,6},{6,7},{7,4},{8,9},{9,10},{10,1... | collective-permute-start | bytes 589832 | tf_op jit(solution)/shard_map/ppermute | solution.py:25
  56.3 98.1 %reduce-scatter.33.cloned.1.call-start = ((), (), s32[]{:S(2)}) async-start(), calls=%async_computation.26 | async-start | bytes 983040 | tf_op jit(solution)/shard_map/reduce_scatter | solution.py:65
  79.9 9.6 %collective-permute-start.12 = (bf16[128,768]{1,0:T(8,128)(2,1)S(1)}, bf16[128,768]{1,0:T(8,128)(2,1)S(1)}, u32[]{:S(2)}, u32[]{:S(2)}) collective-permute-start(bf16[128,768]{1,0:T(8,128)(2,1)S(1)} %fusion.148), channel_id=1, source_target_pairs={{0,1},{1,2},{2,3},{3,0},{4,5},{5,6},{6,7},{7,4},{8,9},{9,10},{10,1... | collective-permute-start | bytes 589832 | tf_op jit(solution)/shard_map/ppermute | solution.py:25
  80.1 10.3 %collective-permute-start.14 = (bf16[128,768]{1,0:T(8,128)(2,1)S(1)}, bf16[128,768]{1,0:T(8,128)(2,1)S(1)}, u32[]{:S(2)}, u32[]{:S(2)}) collective-permute-start(bf16[128,768]{1,0:T(8,128)(2,1)S(1)} %fusion.148), channel_id=1, source_target_pairs={{1,0},{2,1},{3,2},{0,3},{5,4},{6,5},{7,6},{4,7},{9,8},{10,9},{11,1... | collective-permute-start | bytes 589832 | tf_op jit(solution)/shard_map/ppermute | solution.py:27
  89.5 7.5 collective-permute-start.13
  106.3 85.3 %all-gather.7.cloned.1.call-start = ((), (), s32[]{:S(2)}) async-start(), calls=%async_computation.21 | async-start | bytes 1327104 | tf_op jit(solution)/shard_map/all_gather | solution.py:139
  106.9 91.5 %all-gather.9.cloned.1.call-start = ((), (), s32[]{:S(2)}) async-start(), calls=%async_computation.22 | async-start | bytes 1327104 | tf_op jit(solution)/shard_map/all_gather | solution.py:140
  107.5 196.6 %reduce-scatter.49.cloned.1.call-start = ((), (), s32[]{:S(2)}) async-start(), calls=%async_computation.34 | async-start | bytes 983040 | tf_op jit(solution)/shard_map/reduce_scatter | solution.py:76
  159.5 9.9 %collective-permute-start.15 = (bf16[128,768]{1,0:T(8,128)(2,1)S(1)}, bf16[128,768]{1,0:T(8,128)(2,1)S(1)}, u32[]{:S(2)}, u32[]{:S(2)}) collective-permute-start(bf16[128,768]{1,0:T(8,128)(2,1)S(1)} %get-tuple-element.154), channel_id=1, source_target_pairs={{0,1},{1,2},{2,3},{3,0},{4,5},{5,6},{6,7},{7,4},{8,9},{9,10},{10,1... | collective-permute-start | bytes 589832 | tf_op jit(solution)/shard_map/ppermute | solution.py:25
  160.9 14.6 %collective-permute-start.17 = (bf16[128,768]{1,0:T(8,128)(2,1)S(1)}, bf16[128,768]{1,0:T(8,128)(2,1)S(1)}, u32[]{:S(2)}, u32[]{:S(2)}) collective-permute-start(bf16[128,768]{1,0:T(8,128)(2,1)S(1)} %get-tuple-element.154), channel_id=1, source_target_pairs={{1,0},{2,1},{3,2},{0,3},{5,4},{6,5},{7,6},{4,7},{9,8},{10,9},{11,1... | collective-permute-start | bytes 589832 | tf_op jit(solution)/shard_map/ppermute | solution.py:27
  164.5 48.2 %collective-permute-start.5 = (bf16[128,768]{1,0:T(8,128)(2,1)}, bf16[128,768]{1,0:T(8,128)(2,1)}, u32[]{:S(2)}, u32[]{:S(2)}) collective-permute-start(bf16[128,768]{1,0:T(8,128)(2,1)} %get-tuple-element.155), channel_id=1, source_target_pairs={{1,0},{2,1},{3,2},{0,3},{5,4},{6,5},{7,6},{4,7},{9,8},{10,9},{11,1... | collective-permute-start | bytes 589832 | tf_op jit(solution)/shard_map/ppermute | solution.py:27
  165.0 39.5 %collective-permute-start.3 = (bf16[128,768]{1,0:T(8,128)(2,1)}, bf16[128,768]{1,0:T(8,128)(2,1)}, u32[]{:S(2)}, u32[]{:S(2)}) collective-permute-start(bf16[128,768]{1,0:T(8,128)(2,1)} %get-tuple-element.155), channel_id=1, source_target_pairs={{0,1},{1,2},{2,3},{3,0},{4,5},{5,6},{6,7},{7,4},{8,9},{9,10},{10,1... | collective-permute-start | bytes 589832 | tf_op jit(solution)/shard_map/ppermute | solution.py:25
  166.6 19.6 %collective-permute-start.6 = (bf16[128,768]{1,0:T(8,128)(2,1)}, bf16[128,768]{1,0:T(8,128)(2,1)S(1)}, u32[]{:S(2)}, u32[]{:S(2)}) collective-permute-start(bf16[128,768]{1,0:T(8,128)(2,1)} %get-tuple-element.143), channel_id=1, source_target_pairs={{0,1},{1,2},{2,3},{3,0},{4,5},{5,6},{6,7},{7,4},{8,9},{9,10},{10,1... | collective-permute-start | bytes 589832 | tf_op jit(solution)/shard_map/ppermute | solution.py:25
  169.4 18.8 %collective-permute-start.16 = (bf16[128,768]{1,0:T(8,128)(2,1)S(1)}, bf16[128,768]{1,0:T(8,128)(2,1)S(1)}, u32[]{:S(2)}, u32[]{:S(2)}) collective-permute-start(bf16[128,768]{1,0:T(8,128)(2,1)S(1)} %collective-permute-done.15), channel_id=1, source_target_pairs={{0,1},{1,2},{2,3},{3,0},{4,5},{5,6},{6,7},{7,4},{8,9},{9,10},{10,1... | collective-permute-start | bytes 589832 | tf_op jit(solution)/shard_map/ppermute | solution.py:25
  175.5 32.4 %collective-permute-start.8 = (bf16[128,768]{1,0:T(8,128)(2,1)}, bf16[128,768]{1,0:T(8,128)(2,1)}, u32[]{:S(2)}, u32[]{:S(2)}) collective-permute-start(bf16[128,768]{1,0:T(8,128)(2,1)} %get-tuple-element.143), channel_id=1, source_target_pairs={{1,0},{2,1},{3,2},{0,3},{5,4},{6,5},{7,6},{4,7},{9,8},{10,9},{11,1... | collective-permute-start | bytes 589832 | tf_op jit(solution)/shard_map/ppermute | solution.py:27
  186.2 21.8 %collective-permute-start.18 = (bf16[128,768]{1,0:T(8,128)(2,1)}, bf16[128,768]{1,0:T(8,128)(2,1)}, u32[]{:S(2)}, u32[]{:S(2)}) collective-permute-start(bf16[128,768]{1,0:T(8,128)(2,1)} %get-tuple-element.142), channel_id=1, source_target_pairs={{0,1},{1,2},{2,3},{3,0},{4,5},{5,6},{6,7},{7,4},{8,9},{9,10},{10,1... | collective-permute-start | bytes 589832 | tf_op jit(solution)/shard_map/ppermute | solution.py:25
  188.3 19.7 %collective-permute-start.7 = (bf16[128,768]{1,0:T(8,128)(2,1)S(1)}, bf16[128,768]{1,0:T(8,128)(2,1)}, u32[]{:S(2)}, u32[]{:S(2)}) collective-permute-start(bf16[128,768]{1,0:T(8,128)(2,1)S(1)} %collective-permute-done.6), channel_id=1, source_target_pairs={{0,1},{1,2},{2,3},{3,0},{4,5},{5,6},{6,7},{7,4},{8,9},{9,10},{10,1... | collective-permute-start | bytes 589832 | tf_op jit(solution)/shard_map/ppermute | solution.py:25
  204.4 99.7 %reduce-scatter.41.cloned.1.call-start = ((), (), s32[]{:S(2)}) async-start(), calls=%async_computation.30 | async-start | bytes 983040 | tf_op jit(solution)/shard_map/reduce_scatter | solution.py:76
  204.5 31.4 %collective-permute-start.20 = (bf16[128,768]{1,0:T(8,128)(2,1)}, bf16[128,768]{1,0:T(8,128)(2,1)}, u32[]{:S(2)}, u32[]{:S(2)}) collective-permute-start(bf16[128,768]{1,0:T(8,128)(2,1)} %get-tuple-element.142), channel_id=1, source_target_pairs={{1,0},{2,1},{3,2},{0,3},{5,4},{6,5},{7,6},{4,7},{9,8},{10,9},{11,1... | collective-permute-start | bytes 589832 | tf_op jit(solution)/shard_map/ppermute | solution.py:27
  207.9 9.5 %collective-permute-start.4 = (bf16[128,768]{1,0:T(8,128)(2,1)}, bf16[128,768]{1,0:T(8,128)(2,1)}, u32[]{:S(2)}, u32[]{:S(2)}) collective-permute-start(bf16[128,768]{1,0:T(8,128)(2,1)} %collective-permute-done.3), channel_id=1, source_target_pairs={{0,1},{1,2},{2,3},{3,0},{4,5},{5,6},{6,7},{7,4},{8,9},{9,10},{10,1... | collective-permute-start | bytes 589832 | tf_op jit(solution)/shard_map/ppermute | solution.py:25
  207.9 27.9 %collective-permute-start.19 = (bf16[128,768]{1,0:T(8,128)(2,1)}, bf16[128,768]{1,0:T(8,128)(2,1)}, u32[]{:S(2)}, u32[]{:S(2)}) collective-permute-start(bf16[128,768]{1,0:T(8,128)(2,1)} %collective-permute-done.18), channel_id=1, source_target_pairs={{0,1},{1,2},{2,3},{3,0},{4,5},{5,6},{6,7},{7,4},{8,9},{9,10},{10,1... | collective-permute-start | bytes 589832 | tf_op jit(solution)/shard_map/ppermute | solution.py:25
  233.3 70.8 %reduce-scatter.29.cloned.1.call-start = ((), (), s32[]{:S(2)}) async-start(), calls=%async_computation.24 | async-start | bytes 983040 | tf_op jit(solution)/shard_map/reduce_scatter | solution.py:65
  247.7 70.6 %reduce-scatter.37.cloned.1.call-start = ((), (), s32[]{:S(2)}) async-start(), calls=%async_computation.28 | async-start | bytes 983040 | tf_op jit(solution)/shard_map/reduce_scatter | solution.py:65
  253.9 89.4 %reduce-scatter.27.cloned.1.call-start = ((), (), s32[]{:S(2)}) async-start(), calls=%async_computation.23 | async-start | bytes 983040 | tf_op jit(solution)/shard_map/reduce_scatter | solution.py:65
  257.6 121.8 %reduce-scatter.35.cloned.1.call-start = ((), (), s32[]{:S(2)}) async-start(), calls=%async_computation.27 | async-start | bytes 983040 | tf_op jit(solution)/shard_map/reduce_scatter | solution.py:65
  304.0 155.2 %reduce-scatter.51.cloned.1.call-start = ((), (), s32[]{:S(2)}) async-start(), calls=%async_computation.35 | async-start | bytes 983040 | tf_op jit(solution)/shard_map/reduce_scatter | solution.py:76
  347.4 62.9 %collective-permute-start.23 = (bf16[128,768]{1,0:T(8,128)(2,1)}, bf16[128,768]{1,0:T(8,128)(2,1)}, u32[]{:S(2)}, u32[]{:S(2)}) collective-permute-start(bf16[128,768]{1,0:T(8,128)(2,1)} %get-tuple-element.137), channel_id=1, source_target_pairs={{1,0},{2,1},{3,2},{0,3},{5,4},{6,5},{7,6},{4,7},{9,8},{10,9},{11,1... | collective-permute-start | bytes 589832 | tf_op jit(solution)/shard_map/ppermute | solution.py:27
  349.3 57.6 %collective-permute-start.21 = (bf16[128,768]{1,0:T(8,128)(2,1)}, bf16[128,768]{1,0:T(8,128)(2,1)}, u32[]{:S(2)}, u32[]{:S(2)}) collective-permute-start(bf16[128,768]{1,0:T(8,128)(2,1)} %get-tuple-element.137), channel_id=1, source_target_pairs={{0,1},{1,2},{2,3},{3,0},{4,5},{5,6},{6,7},{7,4},{8,9},{9,10},{10,1... | collective-permute-start | bytes 589832 | tf_op jit(solution)/shard_map/ppermute | solution.py:25
  349.4 70.9 %collective-permute-start.11 = (bf16[128,768]{1,0:T(8,128)(2,1)}, bf16[128,768]{1,0:T(8,128)(2,1)}, u32[]{:S(2)}, u32[]{:S(2)}) collective-permute-start(bf16[128,768]{1,0:T(8,128)(2,1)} %get-tuple-element.136), channel_id=1, source_target_pairs={{1,0},{2,1},{3,2},{0,3},{5,4},{6,5},{7,6},{4,7},{9,8},{10,9},{11,1... | collective-permute-start | bytes 589832 | tf_op jit(solution)/shard_map/ppermute | solution.py:27
  353.1 53.8 %collective-permute-start.9 = (bf16[128,768]{1,0:T(8,128)(2,1)}, bf16[128,768]{1,0:T(8,128)(2,1)}, u32[]{:S(2)}, u32[]{:S(2)}) collective-permute-start(bf16[128,768]{1,0:T(8,128)(2,1)} %get-tuple-element.136), channel_id=1, source_target_pairs={{0,1},{1,2},{2,3},{3,0},{4,5},{5,6},{6,7},{7,4},{8,9},{9,10},{10,1... | collective-permute-start | bytes 589832 | tf_op jit(solution)/shard_map/ppermute | solution.py:25
  406.9 8.4 collective-permute-start.22
  406.9 13.3 %collective-permute-start.10 = (bf16[128,768]{1,0:T(8,128)(2,1)}, bf16[128,768]{1,0:T(8,128)(2,1)}, u32[]{:S(2)}, u32[]{:S(2)}) collective-permute-start(bf16[128,768]{1,0:T(8,128)(2,1)} %collective-permute-done.9), channel_id=1, source_target_pairs={{0,1},{1,2},{2,3},{3,0},{4,5},{5,6},{6,7},{7,4},{8,9},{9,10},{10,1... | collective-permute-start | bytes 589832 | tf_op jit(solution)/shard_map/ppermute | solution.py:25
  410.1 49.2 %reduce-scatter.53.cloned.1.call-start = ((), (), s32[]{:S(2)}) async-start(), calls=%async_computation.36 | async-start | bytes 983040 | tf_op jit(solution)/shard_map/reduce_scatter | solution.py:76
  436.2 48.1 %reduce-scatter.45.cloned.1.call-start = ((), (), s32[]{:S(2)}) async-start(), calls=%async_computation.32 | async-start | bytes 983040 | tf_op jit(solution)/shard_map/reduce_scatter | solution.py:76
  447.1 62.0 %reduce-scatter.31.cloned.1.call-start = ((), (), s32[]{:S(2)}) async-start(), calls=%async_computation.25 | async-start | bytes 983040 | tf_op jit(solution)/shard_map/reduce_scatter | solution.py:65
  450.7 83.5 %reduce-scatter.39.cloned.1.call-start = ((), (), s32[]{:S(2)}) async-start(), calls=%async_computation.29 | async-start | bytes 983040 | tf_op jit(solution)/shard_map/reduce_scatter | solution.py:65
  456.6 205.9 %reduce-scatter.63.cloned.1.call-start = ((), (), s32[]{:S(2)}) async-start(), calls=%async_computation.41 | async-start | bytes 884736
  598.5 65.7 %reduce-scatter.43.cloned.1.call-start = ((), (), s32[]{:S(2)}) async-start(), calls=%async_computation.31 | async-start | bytes 983040 | tf_op jit(solution)/shard_map/reduce_scatter | solution.py:76
  605.3 80.4 %reduce-scatter.47.cloned.1.call-start = ((), (), s32[]{:S(2)}) async-start(), calls=%async_computation.33 | async-start | bytes 983040 | tf_op jit(solution)/shard_map/reduce_scatter | solution.py:76
  613.7 96.9 %reduce-scatter.55.cloned.1.call-start = ((), (), s32[]{:S(2)}) async-start(), calls=%async_computation.37 | async-start | bytes 983040 | tf_op jit(solution)/shard_map/reduce_scatter | solution.py:76
  621.3 143.4 %reduce-scatter.61.cloned.1.call-start = ((), (), s32[]{:S(2)}) async-start(), calls=%async_computation.40 | async-start | bytes 2211840
  636.2 163.2 %reduce-scatter.57.cloned.1.call-start = ((), (), s32[]{:S(2)}) async-start(), calls=%async_computation.38 | async-start | bytes 2654208 | tf_op jit(solution)/shard_map/reduce_scatter | solution.py:236
  643.8 201.6 %reduce-scatter.59.cloned.1.call-start = ((), (), s32[]{:S(2)}) async-start(), calls=%async_computation.39 | async-start | bytes 2654208 | tf_op jit(solution)/shard_map/reduce_scatter | solution.py:237
  659.3 51.3 %copy-start.52 = (bf16[128,768]{1,0:T(8,128)(2,1)S(1)}, bf16[128,768]{1,0:T(8,128)(2,1)}, u32[]{:S(2)}) copy-start(bf16[128,768]{1,0:T(8,128)(2,1)} %reduce-scatter.51.cloned.1.call-done) | copy-start | bytes 589828
  659.3 51.3 %copy-start.156 = (f32[128]{0:T(128)S(1)}, f32[128]{0:T(128)}, u32[]{:S(2)}) copy-start(f32[128]{0:T(128)} %copy-done.155) | copy-start | bytes 1540
  659.3 51.3 %copy-start.158 = (f32[128]{0:T(128)S(1)}, f32[128]{0:T(128)}, u32[]{:S(2)}) copy-start(f32[128]{0:T(128)} %copy-done.157) | copy-start | bytes 1540
  659.3 51.3 %copy-start.161 = (f32[128]{0:T(128)S(1)}, f32[128]{0:T(128)}, u32[]{:S(2)}) copy-start(f32[128]{0:T(128)} %copy-done.160) | copy-start | bytes 1540
  659.3 51.3 %copy-start.163 = (f32[128]{0:T(128)S(1)}, f32[128]{0:T(128)}, u32[]{:S(2)}) copy-start(f32[128]{0:T(128)} %copy-done.162) | copy-start | bytes 1540
  659.3 51.3 %copy-start.183 = (f32[128]{0:T(128)S(1)}, f32[128]{0:T(128)}, u32[]{:S(2)}) copy-start(f32[128]{0:T(128)} %copy-done.182) | copy-start | bytes 1540
  659.4 51.3 %copy-start.202 = (f32[128]{0:T(128)S(1)}, f32[128]{0:T(128)}, u32[]{:S(2)}) copy-start(f32[128]{0:T(128)} %multiply_multiply_fusion.22) | copy-start | bytes 1540
  661.8 51.1 %copy-start.213 = (f32[128]{0:T(128)S(1)}, f32[128]{0:T(128)}, u32[]{:S(2)}) copy-start(f32[128]{0:T(128)} %copy-done.212) | copy-start | bytes 1540
  661.8 51.1 %copy-start.211 = (f32[128]{0:T(128)S(1)}, f32[128]{0:T(128)}, u32[]{:S(2)}) copy-start(f32[128]{0:T(128)} %copy-done.210) | copy-start | bytes 1540
  661.8 51.2 %copy-start.218 = (f32[128]{0:T(128)S(1)}, f32[128]{0:T(128)}, u32[]{:S(2)}) copy-start(f32[128]{0:T(128)} %copy-done.217) | copy-start | bytes 1540
  661.8 52.3 %copy-start.181 = (f32[128]{0:T(128)S(1)}, f32[128]{0:T(128)}, u32[]{:S(2)}) copy-start(f32[128]{0:T(128)} %copy-done.180) | copy-start | bytes 1540
  661.8 52.3 %copy-start.186 = (f32[128]{0:T(128)S(1)}, f32[128]{0:T(128)}, u32[]{:S(2)}) copy-start(f32[128]{0:T(128)} %copy-done.185) | copy-start | bytes 1540
  661.9 52.3 %copy-start.188 = (f32[128]{0:T(128)S(1)}, f32[128]{0:T(128)}, u32[]{:S(2)}) copy-start(f32[128]{0:T(128)} %copy-done.187) | copy-start | bytes 1540
  661.9 99.1 %copy-start.37 = (f32[128,768]{1,0:T(8,128)S(1)}, f32[128,768]{1,0:T(8,128)}, u32[]{:S(2)}) copy-start(f32[128,768]{1,0:T(8,128)} %copy-done.36) | copy-start | bytes 1179652
  661.9 99.1 %copy-start.39 = (f32[128,768]{1,0:T(8,128)S(1)}, f32[128,768]{1,0:T(8,128)}, u32[]{:S(2)}) copy-start(f32[128,768]{1,0:T(8,128)} %copy-done.38) | copy-start | bytes 1179652
  (220 other events, 1620.5 us)
Sparse Core Ops, SparseCore 0:
  56.4 22.0 reduce-scatter.24
  106.4 31.0 reduce-scatter.32
  204.5 27.0 reduce-scatter.48
  233.7 25.7 reduce-scatter.40
  261.7 31.2 reduce-scatter.28
  295.2 22.9 reduce-scatter.36
  320.5 22.6 reduce-scatter.26
  345.6 33.7 reduce-scatter.34
  410.2 23.6 reduce-scatter.50
  436.6 22.6 reduce-scatter.52
  461.6 22.6 reduce-scatter.44
  486.4 22.6 reduce-scatter.30
  511.4 22.6 reduce-scatter.38
Sparse Core Ops, SparseCore 1:
  108.6 21.9 all-gather.6
  132.4 23.8 all-gather.8
  598.5 35.8 reduce-scatter.62
  637.3 23.2 reduce-scatter.42
  662.9 22.7 reduce-scatter.46
  687.9 22.6 reduce-scatter.54
  713.9 39.5 reduce-scatter.60
  757.2 42.1 reduce-scatter.56
  803.2 42.2 reduce-scatter.58
